TPU v7x, 32 devices: a whole 2x2x4 slice. The times are simulated.
32 devices in a mesh: wide: 8 (over z, x), narrow: 4 (over y, core).
Axes of the slice: x: 2, y: 2, z: 4, core: 2. Of those that a mesh axis runs over, the one named last changes fastest.
Arguments:
- tokens: bfloat16 [4096, 1024], P(('wide', 'narrow')), may hold values from -6 to 6
- cotangent: bfloat16 [4096, 1024], P(('wide', 'narrow')), may hold values from -0.0625 to 0.0625
- segment_ids: int32 [32, 128], P(('wide', 'narrow')), may hold values from 0 to 7, never falling along the last dimension, each value on 1 to 32 neighbouring positions
- w_qkv: float32 [1024, 3072], P(('wide', 'narrow')), may hold values from -0.1875 to 0.1875
- w_out: float32 [1024, 1024], P(('wide', 'narrow')), may hold values from -0.375 to 0.375
- w_up: float32 [1024, 4096], P(('wide', 'narrow')), may hold values from -0.1875 to 0.1875
- w_down: float32 [4096, 1024], P(('wide', 'narrow')), may hold values from -0.09375 to 0.09375
- vectors: float32 [1024, 12], P(('wide', 'narrow')), as said below
- moments_qkv: float32 [2, 1024, 3072], P(None, ('wide', 'narrow')), as said below
- moments_out: float32 [2, 1024, 1024], P(None, ('wide', 'narrow')), as said below
- moments_up: float32 [2, 1024, 4096], P(None, ('wide', 'narrow')), as said below
- moments_down: float32 [2, 4096, 1024], P(None, ('wide', 'narrow')), as said below
- moments_vec: float32 [2, 1024, 12], P(None, ('wide', 'narrow')), as said below
Outputs:
- block_out: bfloat16 [4096, 1024], P(('wide', 'narrow'))
- input_grad: float32 [4096, 1024], P(('wide', 'narrow'))
- new_qkv: float32 [1024, 3072], P(('wide', 'narrow'))
- new_out: float32 [1024, 1024], P(('wide', 'narrow'))
- new_up: float32 [1024, 4096], P(('wide', 'narrow'))
- new_down: float32 [4096, 1024], P(('wide', 'narrow'))
- new_vectors: float32 [1024, 12], P(('wide', 'narrow'))
- state_qkv: float32 [2, 1024, 3072], P(None, ('wide', 'narrow'))
- state_out: float32 [2, 1024, 1024], P(None, ('wide', 'narrow'))
- state_up: float32 [2, 1024, 4096], P(None, ('wide', 'narrow'))
- state_down: float32 [2, 4096, 1024], P(None, ('wide', 'narrow'))
- state_vectors: float32 [2, 1024, 12], P(None, ('wide', 'narrow'))
- copy_qkv: bfloat16 [1024, 3072], P(('wide', 'narrow'))
- copy_out: bfloat16 [1024, 1024], P(('wide', 'narrow'))
- copy_up: bfloat16 [1024, 4096], P(('wide', 'narrow'))
- copy_down: bfloat16 [4096, 1024], P(('wide', 'narrow'))
- copy_vectors: bfloat16 [1024, 12], P(('wide', 'narrow'))
Inputs may be any that keep to these rules, and one draw needn't show every extreme that they name: `segment_ids`: in each sequence the ids never fall, every id is used, each segment has 1 to 32 patches and one has exactly 32. `vectors`: columns 0 and 5 are positive gains; the others are biases of both signs. `moments_qkv`: the second slice is positive. `moments_out`: the second slice is positive. `moments_up`: the second slice is positive. `moments_down`: the second slice is positive. `moments_vec`: the second slice is positive.
All inputs are finite; a program needn't handle non-finite values.
Results may differ from a plain program's by a relative error of at most 0.02.
Values may be sent and summed in bfloat16 or wider, within the bound.
A program may use at most 256 MiB of HBM per device.

v0:
```python
import jax
import jax.numpy as jnp
from jax import lax
from jax.sharding import PartitionSpec as P

D = 1024
HEADS = 16
FF = 4096
STEP = 3
NORM_EPSILON = 1e-06
MASK_VALUE = -1e30
MOMENT_DECAY = 0.5
RATE_MATRIX = 0.04
RATE_VECTOR = 0.2
WEIGHT_DECAY = 0.1
ADAM_EPSILON = 1e-08


def layer_norm(values, scale_row, offset_row):
    center = values - jnp.mean(values, axis=-1, keepdims=True)
    spread = jnp.mean(center * center, axis=-1, keepdims=True)
    return center * lax.rsqrt(spread + NORM_EPSILON) * scale_row + offset_row


def exact_gelu(values):
    return jax.nn.gelu(values, approximate=False)


def adam_update(master, moments, gradient, rate, decay):
    first_moment = MOMENT_DECAY * moments[0] + (1.0 - MOMENT_DECAY) * gradient
    second_moment = MOMENT_DECAY * moments[1] + (1.0 - MOMENT_DECAY) * gradient * gradient
    correction = 1.0 - MOMENT_DECAY**STEP
    normalized = first_moment / correction / (jnp.sqrt(second_moment / correction) + ADAM_EPSILON)
    updated = master - rate * (normalized + decay * master)
    return (updated, jnp.stack([first_moment, second_moment]), updated.astype(jnp.bfloat16))


def unpack_vectors(packed):
    columns = [packed[:, column] for column in range(8)]
    columns.append(packed[:, 8:].T.reshape(FF))
    return columns


def body(
    tokens,
    cotangent,
    segment_ids,
    w_qkv,
    w_out,
    w_up,
    w_down,
    vectors,
    moments_qkv,
    moments_out,
    moments_up,
    moments_down,
    moments_vec,
):
    qkv_low = w_qkv.astype(jnp.bfloat16)
    out_low = w_out.astype(jnp.bfloat16)
    up_low = w_up.astype(jnp.bfloat16)
    down_low = w_down.astype(jnp.bfloat16)
    vec_low = vectors.astype(jnp.bfloat16)
    gathered = (
        lax.all_gather(qkv_low, ("wide", "narrow"), axis=0, tiled=True),
        lax.all_gather(out_low, ("wide", "narrow"), axis=0, tiled=True),
        lax.all_gather(up_low, ("wide", "narrow"), axis=0, tiled=True),
        lax.all_gather(down_low, ("wide", "narrow"), axis=0, tiled=True),
        lax.all_gather(vec_low, ("wide", "narrow"), axis=0, tiled=True),
    )
    qkv_full, out_full, up_full, down_full, vec_full = gathered
    length = tokens.shape[0]
    block_rows = min(512, length)
    block_count = length // block_rows
    head_dim = D // HEADS
    scale_value = head_dim ** (-0.5)
    segments = segment_ids[0]
    (
        gain_one,
        shift_one,
        bias_query,
        bias_value,
        bias_out,
        gain_two,
        shift_two,
        bias_down,
        bias_up,
    ) = unpack_vectors(vec_full.astype(jnp.float32))
    inputs = tokens.astype(jnp.float32)
    normed_one = layer_norm(inputs, gain_one, shift_one).astype(jnp.bfloat16)
    qkv_bias = jnp.concatenate([bias_query, jnp.zeros_like(bias_query), bias_value])
    qkv_value = (
        jnp.dot(normed_one, qkv_full, preferred_element_type=jnp.float32) + qkv_bias
    ).astype(jnp.bfloat16)
    queries = qkv_value[:, :D].reshape(length, HEADS, head_dim)
    keys_all = qkv_value[:, D : 2 * D].reshape(length, HEADS, head_dim)
    values_all = qkv_value[:, 2 * D :].reshape(length, HEADS, head_dim)
    query_blocks = queries.reshape(block_count, block_rows, HEADS, head_dim)
    segment_blocks = segments.reshape(block_count, block_rows)

    def masked_scores(query_block, segment_block):
        raw_scores = (
            jnp.einsum("qhd,khd->hqk", query_block, keys_all, preferred_element_type=jnp.float32)
            * scale_value
        )
        same_segment = segment_block[:, None] == segments[None, :]
        return jnp.where(same_segment[None], raw_scores, MASK_VALUE)

    def attend(pieces):
        query_block, segment_block = pieces
        scores = masked_scores(query_block, segment_block)
        highest = jnp.max(scores, axis=-1, keepdims=True)
        exp_scores = jnp.exp(scores - highest)
        totals = jnp.sum(exp_scores, axis=-1, keepdims=True)
        soft_weights = (exp_scores / totals).astype(jnp.bfloat16)
        mixed = jnp.einsum(
            "hqk,khd->qhd", soft_weights, values_all, preferred_element_type=jnp.float32
        )
        return (mixed.astype(jnp.bfloat16), (highest + jnp.log(totals))[:, :, 0])

    attended, log_totals = lax.map(attend, (query_blocks, segment_blocks))
    attended = attended.reshape(length, D)
    resid_one = inputs + jnp.dot(attended, out_full, preferred_element_type=jnp.float32) + bias_out
    normed_two = layer_norm(resid_one, gain_two, shift_two).astype(jnp.bfloat16)
    hidden_pre = jnp.dot(normed_two, up_full, preferred_element_type=jnp.float32) + bias_up
    hidden_act, gelu_pull = jax.vjp(exact_gelu, hidden_pre)
    hidden_low = hidden_act.astype(jnp.bfloat16)
    block_out = (
        resid_one + jnp.dot(hidden_low, down_full, preferred_element_type=jnp.float32) + bias_down
    ).astype(jnp.bfloat16)
    back_weights = (
        lax.all_gather(qkv_low, ("wide", "narrow"), axis=0, tiled=True),
        lax.all_gather(out_low, ("wide", "narrow"), axis=0, tiled=True),
        lax.all_gather(up_low, ("wide", "narrow"), axis=0, tiled=True),
        lax.all_gather(down_low, ("wide", "narrow"), axis=0, tiled=True),
        lax.all_gather(vec_low, ("wide", "narrow"), axis=0, tiled=True),
    )
    qkv_back, out_back, up_back, down_back, vec_back = back_weights
    back_params = unpack_vectors(vec_back.astype(jnp.float32))
    grad_down = jnp.einsum("sf,sd->fd", hidden_low, cotangent, preferred_element_type=jnp.float32)
    grad_bias_down = jnp.sum(cotangent.astype(jnp.float32), axis=0)
    grad_hidden = jnp.einsum("sd,fd->sf", cotangent, down_back, preferred_element_type=jnp.float32)
    grad_pre = gelu_pull(grad_hidden)[0].astype(jnp.bfloat16)
    grad_up = jnp.einsum("sd,sf->df", normed_two, grad_pre, preferred_element_type=jnp.float32)
    grad_bias_up = jnp.sum(grad_pre.astype(jnp.float32), axis=0)
    grad_normed_two = jnp.einsum("sf,df->sd", grad_pre, up_back, preferred_element_type=jnp.float32)
    norm_value_two, norm_pull_two = jax.vjp(layer_norm, resid_one, back_params[5], back_params[6])
    part_resid, grad_gain_two, grad_shift_two = norm_pull_two(grad_normed_two)
    grad_resid = cotangent.astype(jnp.float32) + part_resid
    grad_branch = grad_resid.astype(jnp.bfloat16)
    grad_out = jnp.einsum("sd,se->de", attended, grad_branch, preferred_element_type=jnp.float32)
    grad_bias_out = jnp.sum(grad_resid, axis=0)
    grad_attended = jnp.einsum(
        "se,de->sd", grad_branch, out_back, preferred_element_type=jnp.float32
    ).astype(jnp.bfloat16)
    grad_blocks = grad_attended.reshape(block_count, block_rows, HEADS, head_dim)

    def attend_back(running, pieces):
        key_grad, value_grad = running
        query_block, segment_block, grad_block, log_block = pieces
        scores = masked_scores(query_block, segment_block)
        soft_weights = jnp.exp(scores - log_block[:, :, None])
        value_grad = value_grad + jnp.einsum(
            "hqk,qhd->khd",
            soft_weights.astype(jnp.bfloat16),
            grad_block,
            preferred_element_type=jnp.float32,
        )
        grad_soft = jnp.einsum(
            "qhd,khd->hqk", grad_block, values_all, preferred_element_type=jnp.float32
        )
        inner_sum = jnp.sum(soft_weights * grad_soft, axis=-1, keepdims=True)
        grad_scores = (soft_weights * (grad_soft - inner_sum)).astype(jnp.bfloat16)
        query_grad = (
            jnp.einsum("hqk,khd->qhd", grad_scores, keys_all, preferred_element_type=jnp.float32)
            * scale_value
        )
        key_grad = (
            key_grad
            + jnp.einsum(
                "hqk,qhd->khd", grad_scores, query_block, preferred_element_type=jnp.float32
            )
            * scale_value
        )
        return ((key_grad, value_grad), query_grad)

    zero_heads = jnp.zeros((length, HEADS, head_dim), jnp.float32)
    (key_grad, value_grad), query_grad = lax.scan(
        attend_back,
        (zero_heads, zero_heads),
        (query_blocks, segment_blocks, grad_blocks, log_totals),
    )
    grad_qkv = jnp.concatenate(
        [query_grad.reshape(length, D), key_grad.reshape(length, D), value_grad.reshape(length, D)],
        axis=1,
    ).astype(jnp.bfloat16)
    grad_qkv_weight = jnp.einsum(
        "sd,sf->df", normed_one, grad_qkv, preferred_element_type=jnp.float32
    )
    qkv_sums = jnp.sum(grad_qkv.astype(jnp.float32), axis=0)
    grad_normed_one = jnp.einsum(
        "sf,df->sd", grad_qkv, qkv_back, preferred_element_type=jnp.float32
    )
    norm_value_one, norm_pull_one = jax.vjp(layer_norm, inputs, back_params[0], back_params[1])
    part_input, grad_gain_one, grad_shift_one = norm_pull_one(grad_normed_one)
    input_grad = grad_resid + part_input
    vector_head = jnp.stack(
        [
            grad_gain_one,
            grad_shift_one,
            qkv_sums[:D],
            qkv_sums[2 * D :],
            grad_bias_out,
            grad_gain_two,
            grad_shift_two,
            grad_bias_down,
        ],
        axis=1,
    )
    vector_grad = jnp.concatenate([vector_head, grad_bias_up.reshape(FF // D, D).T], axis=1)
    wide_count = lax.axis_size("wide")
    narrow_count = lax.axis_size("narrow")

    def split_rows(gradient):
        return gradient.reshape(
            wide_count,
            narrow_count,
            gradient.shape[0] // (wide_count * narrow_count),
            gradient.shape[1],
        )

    group_sums = (
        lax.psum_scatter(
            split_rows(grad_qkv_weight).astype(jnp.bfloat16),
            "narrow",
            scatter_dimension=1,
            tiled=True,
        ).astype(jnp.float32),
        lax.psum_scatter(
            split_rows(grad_out).astype(jnp.bfloat16), "narrow", scatter_dimension=1, tiled=True
        ).astype(jnp.float32),
        lax.psum_scatter(
            split_rows(grad_up).astype(jnp.bfloat16), "narrow", scatter_dimension=1, tiled=True
        ).astype(jnp.float32),
        lax.psum_scatter(
            split_rows(grad_down).astype(jnp.bfloat16), "narrow", scatter_dimension=1, tiled=True
        ).astype(jnp.float32),
        lax.psum_scatter(
            split_rows(vector_grad).astype(jnp.bfloat16), "narrow", scatter_dimension=1, tiled=True
        ).astype(jnp.float32),
    )
    owned_sums = (
        lax.psum_scatter(
            group_sums[0].astype(jnp.bfloat16), "wide", scatter_dimension=0, tiled=True
        ).astype(jnp.float32),
        lax.psum_scatter(
            group_sums[1].astype(jnp.bfloat16), "wide", scatter_dimension=0, tiled=True
        ).astype(jnp.float32),
        lax.psum_scatter(
            group_sums[2].astype(jnp.bfloat16), "wide", scatter_dimension=0, tiled=True
        ).astype(jnp.float32),
        lax.psum_scatter(
            group_sums[3].astype(jnp.bfloat16), "wide", scatter_dimension=0, tiled=True
        ).astype(jnp.float32),
        lax.psum_scatter(
            group_sums[4].astype(jnp.bfloat16), "wide", scatter_dimension=0, tiled=True
        ).astype(jnp.float32),
    )
    reduced = tuple((member.reshape(member.shape[2], member.shape[3]) for member in owned_sums))
    new_qkv, state_qkv, copy_qkv = adam_update(
        w_qkv, moments_qkv, reduced[0], RATE_MATRIX, WEIGHT_DECAY
    )
    new_out, state_out, copy_out = adam_update(
        w_out, moments_out, reduced[1], RATE_MATRIX, WEIGHT_DECAY
    )
    new_up, state_up, copy_up = adam_update(w_up, moments_up, reduced[2], RATE_MATRIX, WEIGHT_DECAY)
    new_down, state_down, copy_down = adam_update(
        w_down, moments_down, reduced[3], RATE_MATRIX, WEIGHT_DECAY
    )
    new_vectors, state_vectors, copy_vectors = adam_update(
        vectors, moments_vec, reduced[4], RATE_VECTOR, 0.0
    )
    return (
        block_out,
        input_grad,
        new_qkv,
        new_out,
        new_up,
        new_down,
        new_vectors,
        state_qkv,
        state_out,
        state_up,
        state_down,
        state_vectors,
        copy_qkv,
        copy_out,
        copy_up,
        copy_down,
        copy_vectors,
    )


def solution(mesh):
    placed = (
        P(("wide", "narrow"), None),
        P(("wide", "narrow"), None),
        P(("wide", "narrow"), None),
        P(("wide", "narrow"), None),
        P(("wide", "narrow"), None),
        P(("wide", "narrow"), None),
        P(("wide", "narrow"), None),
        P(("wide", "narrow"), None),
        P(None, ("wide", "narrow"), None),
        P(None, ("wide", "narrow"), None),
        P(None, ("wide", "narrow"), None),
        P(None, ("wide", "narrow"), None),
        P(None, ("wide", "narrow"), None),
    )
    return jax.shard_map(
        body,
        mesh=mesh,
        in_specs=placed,
        out_specs=(
            P(("wide", "narrow"), None),
            P(("wide", "narrow"), None),
            P(("wide", "narrow"), None),
            P(("wide", "narrow"), None),
            P(("wide", "narrow"), None),
            P(("wide", "narrow"), None),
            P(("wide", "narrow"), None),
            P(None, ("wide", "narrow"), None),
            P(None, ("wide", "narrow"), None),
            P(None, ("wide", "narrow"), None),
            P(None, ("wide", "narrow"), None),
            P(None, ("wide", "narrow"), None),
            P(("wide", "narrow"), None),
            P(("wide", "narrow"), None),
            P(("wide", "narrow"), None),
            P(("wide", "narrow"), None),
            P(("wide", "narrow"), None),
        ),
        check_vma=False,
    )
```

profile of v0, /device:TPU:0, one launch (start us, length us, event | category | flops | bytes accessed | tf_op | source)
XLA Modules:
  0.0 1126.8 jit_solution(3805992562656520872)
XLA Ops:
  7.3 1.8 convert_element_type.142
  9.1 1.5 convert_element_type.147
  10.7 1.8 convert_element_type.149
  12.6 0.7 convert_element_type.151
  13.6 43.8 %all-gather = bf16[32,32,12]{1,2,0:T(8,128)(2,1)S(1)} all-gather(bf16[1,32,12]{1,2,0:T(8,128)(2,1)S(1)} %convert_bitcast_fusion.10), channel_id=1, replica_groups=mesh['wide'=8,'narrow'=4] {'wide','narrow'}, dimensions={0}, use_global_device_ids=true | all-gather | bytes 25344 | tf_op jit(solution)/shard_map/all_gather | solution.py:69
  58.1 25.6 %all-gather.6.cloned.1.call-done = bf16[1024,3072]{1,0:T(8,128)(2,1)} async-done(((bf16[32,3072]{1,0:T(8,128)(2,1)}), bf16[1024,3072]{1,0:T(8,128)(2,1)}) %all-gather.6.cloned.1.call-update) | async-done | bytes 6291472 | tf_op jit(solution)/shard_map/all_gather | solution.py:65
  83.7 3.9 fusion
  88.2 0.4 fusion.109
  88.7 0.3 convolution_convert_fusion.6
  89.1 52.9 %all-gather.8.cloned.1.call-done = bf16[1024,1024]{1,0:T(8,128)(2,1)} async-done(((bf16[32,1024]{1,0:T(8,128)(2,1)}), bf16[1024,1024]{1,0:T(8,128)(2,1)}) %all-gather.8.cloned.1.call-update) | async-done | bytes 2097168 | tf_op jit(solution)/shard_map/all_gather | solution.py:66
  141.9 2.1 fusion.110
  144.3 77.0 %all-gather.10.cloned.1.call-done = bf16[1024,4096]{1,0:T(8,128)(2,1)} async-done(((bf16[32,4096]{1,0:T(8,128)(2,1)}), bf16[1024,4096]{1,0:T(8,128)(2,1)}) %all-gather.10.cloned.1.call-update) | async-done | bytes 8388624 | tf_op jit(solution)/shard_map/all_gather | solution.py:67
  221.3 6.1 convolution_add_fusion
  227.4 72.9 %all-gather.12.cloned.1.call-done = bf16[4096,1024]{1,0:T(8,128)(2,1)} async-done(((bf16[128,1024]{1,0:T(8,128)(2,1)}), bf16[4096,1024]{1,0:T(8,128)(2,1)}) %all-gather.12.cloned.1.call-update) | async-done | bytes 8388624 | tf_op jit(solution)/shard_map/all_gather | solution.py:68
  300.3 10.9 fusion.102
  311.2 3.0 multiply_reduce_fusion.1
  314.2 0.3 fusion.104
  314.5 0.8 convolution_convert_fusion.5
  315.6 0.5 convolution_convert_fusion.4
  316.0 1.3 multiply_reduce_fusion
  317.6 0.5 fusion.12
  318.1 0.2 copy-done.11
  318.3 0.3 fusion.11
  318.6 0.3 fusion.87
  318.9 4.7 convolution_convert_fusion.2
  323.6 5.7 convolution_convert_fusion.1
  329.8 5.1 fusion.91
  334.9 0.4 fusion.23
  335.2 1.1 fusion.90
  336.9 0.7 copy.95
  337.6 0.3 all-reduce.7.cloned.1.call-start
  337.9 5.6 convolution_convert_fusion
  343.4 2.1 convolution_convert_fusion.3
  345.6 0.6 copy-done.28
  346.2 0.6 dynamic-slice
  346.8 9.2 reduce-scatter.27.cloned.1.call-done
  356.0 1.4 copy.96
  357.4 424.2 %all-reduce.7.cloned.1.call-done = (bf16[8,4,32,3072]{3,2,1,0:T(8,128)(2,1)}, bf16[8,4,32,1024]{3,2,1,0:T(8,128)(2,1)}, bf16[8,4,32,4096]{3,2,1,0:T(8,128)(2,1)}, bf16[8,4,128,1024]{3,2,1,0:T(8,128)(2,1)}) async-done(((bf16[8,4,32,3072]{3,2,1,0:T(8,128)(2,1)}, bf16[8,4,32,1024]{3,2,1,0:T(8,128)(2,1)}, bf16[8,4,32,4096]{3,2,1,0:T(8,128)(2,1)}, bf16[8,4,128,1024]{3,2,1,0:T(8,128)(2,1)}), ...) | async-done | bytes 25165840
  781.6 2.5 constant_dynamic-slice_fusion.2
  784.2 3.3 constant_dynamic-slice_fusion.3
  787.6 3.8 constant_dynamic-slice_fusion.1
  791.5 0.6 copy-done.26
  792.1 5.4 fusion.10
  797.5 3.8 constant_dynamic-slice_fusion
  801.3 39.0 %reduce-scatter.29.cloned.1.call-done = bf16[1,1,32,12]{2,3,1,0:T(8,128)(2,1)} async-done(((bf16[8,1,32,12]{2,3,1,0:T(8,128)(2,1)}), bf16[1,1,32,12]{2,3,1,0:T(8,128)(2,1)}) %reduce-scatter.29.cloned.1.call-update) | async-done | bytes 784 | tf_op jit(solution)/shard_map/reduce_scatter | solution.py:265
  840.3 0.7 multiply_add_fusion.8
  841.0 0.6 copy.100
  841.6 1.3 fusion.92
  842.9 63.0 %reduce-scatter.21.cloned.1.call-done = bf16[1,1,32,1024]{3,2,1,0:T(8,128)(2,1)} async-done(((bf16[8,1,32,1024]{3,2,1,0:T(8,128)(2,1)}), bf16[1,1,32,1024]{3,2,1,0:T(8,128)(2,1)}) %reduce-scatter.21.cloned.1.call-update) | async-done | bytes 65552 | tf_op jit(solution)/shard_map/reduce_scatter | solution.py:256
  905.9 0.9 multiply_add_fusion.6
  906.7 0.7 pad_maximum_fusion.4
  907.5 1.7 fusion.98
  909.2 64.7 %reduce-scatter.19.cloned.1.call-done = bf16[1,1,32,3072]{3,2,1,0:T(8,128)(2,1)} async-done(((bf16[8,1,32,3072]{3,2,1,0:T(8,128)(2,1)}), bf16[1,1,32,3072]{3,2,1,0:T(8,128)(2,1)}) %reduce-scatter.19.cloned.1.call-update) | async-done | bytes 196624 | tf_op jit(solution)/shard_map/reduce_scatter | solution.py:253
  973.8 1.1 multiply_add_fusion.4
  975.0 0.9 pad_maximum_fusion.3
  975.9 1.1 fusion.100
  977.0 67.6 %reduce-scatter.23.cloned.1.call-done = bf16[1,1,32,4096]{3,2,1,0:T(8,128)(2,1)} async-done(((bf16[8,1,32,4096]{3,2,1,0:T(8,128)(2,1)}), bf16[1,1,32,4096]{3,2,1,0:T(8,128)(2,1)}) %reduce-scatter.23.cloned.1.call-update) | async-done | bytes 262160 | tf_op jit(solution)/shard_map/reduce_scatter | solution.py:259
  1044.6 1.1 multiply_add_fusion.1
  1045.7 1.0 pad_maximum_fusion
  1046.7 68.8 %reduce-scatter.25.cloned.1.call-done = bf16[1,1,128,1024]{3,2,1,0:T(8,128)(2,1)} async-done(((bf16[8,1,128,1024]{3,2,1,0:T(8,128)(2,1)}), bf16[1,1,128,1024]{3,2,1,0:T(8,128)(2,1)}) %reduce-scatter.25.cloned.1.call-update) | async-done | bytes 262160 | tf_op jit(solution)/shard_map/reduce_scatter | solution.py:262
  1115.5 1.1 multiply_add_fusion
  1116.6 1.1 pad_maximum_fusion.1
  1117.7 1.3 fusion.96
  1119.0 1.3 fusion.94
  (128 shorter events, 3.9 us)
Async XLA Ops:
  7.2 5.4 copy-start.13
  7.2 6.2 copy-start.4
  7.2 6.4 copy-start.25
  7.2 50.4 %copy-start.1 = (bf16[128,1024]{1,0:T(8,128)(2,1)S(1)}, bf16[128,1024]{1,0:T(8,128)(2,1)}, u32[]{:S(2)}) copy-start(bf16[128,1024]{1,0:T(8,128)(2,1)} %param.13) | copy-start | bytes 786436
  7.2 76.4 %all-gather.6.cloned.1.call-start = ((), (), s32[]{:S(2)}) async-start(), calls=%async_computation.6 | async-start | bytes 6488064 | tf_op jit(solution)/shard_map/all_gather | solution.py:65
  9.0 48.9 %copy-start.27 = (s32[1,128]{1,0:T(1,128)S(1)}, s32[1,128]{1,0:T(1,128)}, u32[]{:S(2)}) copy-start(s32[1,128]{1,0:T(1,128)} %param.15) | copy-start | bytes 1540
  9.1 132.8 %all-gather.8.cloned.1.call-start = ((), (), s32[]{:S(2)}) async-start(), calls=%async_computation.7 | async-start | bytes 2162688 | tf_op jit(solution)/shard_map/all_gather | solution.py:66
  10.7 210.6 %all-gather.10.cloned.1.call-start = ((), (), s32[]{:S(2)}) async-start(), calls=%async_computation.8 | async-start | bytes 8650752 | tf_op jit(solution)/shard_map/all_gather | solution.py:67
  12.5 287.8 %all-gather.12.cloned.1.call-start = ((), (), s32[]{:S(2)}) async-start(), calls=%async_computation.9 | async-start | bytes 8650752 | tf_op jit(solution)/shard_map/all_gather | solution.py:68
  13.4 342.6 %reduce-scatter.27.cloned.1.call-start = ((), (), s32[]{:S(2)}) async-start(), calls=%async_computation.14 | async-start | bytes 122880 | tf_op jit(solution)/shard_map/reduce_scatter | solution.py:248
  87.8 1.2 copy-start.10
  88.2 0.9 copy-start.19
  89.0 138.3 %copy-start.21 = (bf16[16,64,128]{2,1,0:T(8,128)(2,1)}, bf16[16,64,128]{2,1,0:T(8,128)(2,1)S(1)}, u32[]{:S(2)}) copy-start(bf16[16,64,128]{2,1,0:T(8,128)(2,1)S(1)} %convolution_convert_fusion.6) | copy-start | bytes 786436
  300.3 10.9 copy-start
  311.2 3.0 copy-start.5
  311.2 3.3 copy-start.3
  317.4 1.0 copy-start.11
  318.9 4.7 copy-start.6
  323.6 5.7 copy-start.2
  323.6 5.7 copy-start.15
  337.6 5.9 copy-start.22
  337.6 444.0 %all-reduce.7.cloned.1.call-start = ((), (), s32[]{:S(2)}) async-start(), calls=%async_computation.16 | async-start | bytes 50331648
  345.6 0.7 copy-start.28
  345.6 494.7 %reduce-scatter.29.cloned.1.call-start = ((), (), s32[]{:S(2)}) async-start(), calls=%async_computation.15 | async-start | bytes 36864 | tf_op jit(solution)/shard_map/reduce_scatter | solution.py:265
  357.4 548.5 %reduce-scatter.21.cloned.1.call-start = ((), (), s32[]{:S(2)}) async-start(), calls=%async_computation.11 | async-start | bytes 589824 | tf_op jit(solution)/shard_map/reduce_scatter | solution.py:256
  784.1 189.7 %reduce-scatter.19.cloned.1.call-start = ((), (), s32[]{:S(2)}) async-start(), calls=%async_computation.10 | async-start | bytes 1769472 | tf_op jit(solution)/shard_map/reduce_scatter | solution.py:253
  787.5 257.1 %reduce-scatter.23.cloned.1.call-start = ((), (), s32[]{:S(2)}) async-start(), calls=%async_computation.12 | async-start | bytes 2359296 | tf_op jit(solution)/shard_map/reduce_scatter | solution.py:259
  791.4 0.7 copy-start.26
  791.4 324.1 %reduce-scatter.25.cloned.1.call-start = ((), (), s32[]{:S(2)}) async-start(), calls=%async_computation.13 | async-start | bytes 2359296 | tf_op jit(solution)/shard_map/reduce_scatter | solution.py:262
  801.2 104.6 %copy-start.20 = (f32[2,32,1024]{2,1,0:T(8,128)S(1)}, f32[2,32,1024]{2,1,0:T(8,128)}, u32[]{:S(2)}) copy-start(f32[2,32,1024]{2,1,0:T(8,128)} %param.22) | copy-start | bytes 786436
  801.2 106.3 %copy-start.24 = (f32[32,1024]{1,0:T(8,128)S(1)}, f32[32,1024]{1,0:T(8,128)}, u32[]{:S(2)}) copy-start(f32[32,1024]{1,0:T(8,128)} %param.17) | copy-start | bytes 393220
  801.2 172.6 %copy-start.9 = (f32[2,32,3072]{2,1,0:T(8,128)S(1)}, f32[2,32,3072]{2,1,0:T(8,128)}, u32[]{:S(2)}) copy-start(f32[2,32,3072]{2,1,0:T(8,128)} %param.21) | copy-start | bytes 2359300
  907.5 68.4 %copy-start.16 = (f32[32,3072]{1,0:T(8,128)S(1)}, f32[32,3072]{1,0:T(8,128)}, u32[]{:S(2)}) copy-start(f32[32,3072]{1,0:T(8,128)} %param.16) | copy-start | bytes 1179652
  973.8 2.0 copy-start.23
  974.9 69.7 %copy-start.7 = (f32[2,32,4096]{2,1,0:T(8,128)S(1)}, f32[2,32,4096]{2,1,0:T(8,128)}, u32[]{:S(2)}) copy-start(f32[2,32,4096]{2,1,0:T(8,128)} %param.23) | copy-start | bytes 3145732
  977.0 138.5 %copy-start.8 = (f32[2,128,1024]{2,1,0:T(8,128)S(1)}, f32[2,128,1024]{2,1,0:T(8,128)}, u32[]{:S(2)}) copy-start(f32[2,128,1024]{2,1,0:T(8,128)} %param.24) | copy-start | bytes 3145732
  1046.7 71.0 %copy-start.12 = (f32[32,4096]{1,0:T(8,128)S(1)}, f32[32,4096]{1,0:T(8,128)}, u32[]{:S(2)}) copy-start(f32[32,4096]{1,0:T(8,128)} %param.18) | copy-start | bytes 1572868
  1046.7 71.0 %copy-start.17 = (bf16[1,1,32,4096]{3,2,1,0:T(8,128)(2,1)S(1)}, bf16[1,1,32,4096]{3,2,1,0:T(8,128)(2,1)}, u32[]{:S(2)}) copy-start(bf16[1,1,32,4096]{3,2,1,0:T(8,128)(2,1)} %reduce-scatter.23.cloned.1.call-done) | copy-start | bytes 786436
  1116.6 2.4 copy-start.14
  1116.6 2.4 copy-start.18
Sparse Core Ops, SparseCore 0:
  11.5 72.1 all-gather.5
  87.1 54.7 all-gather.7
  145.4 75.9 all-gather.9
  224.6 75.6 all-gather.11
  337.7 18.2 reduce-scatter.26
  358.6 422.9 all-reduce.6
  785.3 54.9 reduce-scatter.28
  844.2 61.6 reduce-scatter.20
  909.3 64.4 reduce-scatter.18
  977.2 67.3 reduce-scatter.22
  1048.1 67.3 reduce-scatter.24
where the time goes:
time: 1130 us
  waiting for transfers between devices  965 us (85%)
  matrix products  58.5 us (5%)
  blocking collectives  43.8 us (4%)
  other arithmetic  24.5 us (2%)
  local copies, waits for them, and re-layouts  19.9 us (2%)
  between operations  14.4 us (1%)
    unnamed x12, waiting for transfers between devices  424 us
    all_gather x1, waiting for transfers between devices, body(): lax.all_gather(up_low, ('wide', 'narrow'), axis=0, tiled=True)  77 us
    all_gather x1, waiting for transfers between devices, body(): lax.all_gather(down_low, ('wide', 'narrow'), axis=0, tiled=True)  72.9 us
    reduce_scatter x1, waiting for transfers between devices, body(): lax.psum_scatter(group_sums[3].astype(jnp.bfloat16), 'wide', scatter_dime...  68.8 us
    reduce_scatter x1, waiting for transfers between devices, body(): lax.psum_scatter(group_sums[2].astype(jnp.bfloat16), 'wide', scatter_dime...  67.6 us
    reduce_scatter x1, waiting for transfers between devices, body(): lax.psum_scatter(group_sums[0].astype(jnp.bfloat16), 'wide', scatter_dime...  64.7 us
    reduce_scatter x1, waiting for transfers between devices, body(): lax.psum_scatter(group_sums[1].astype(jnp.bfloat16), 'wide', scatter_dime...  63 us
    all_gather x1, waiting for transfers between devices, body(): lax.all_gather(out_low, ('wide', 'narrow'), axis=0, tiled=True)  52.9 us
  transfers between devices with their start and end apart: 11, of which 11 were waited for; matrix products, arithmetic and copies ran while one was open for 5% of the time, Pallas kernels for 0%

commit v1 on v0

--- a/solution.py
+++ b/solution.py
@@ -64,7 +64,12 @@
     gathered = (
         lax.all_gather(qkv_low, ("wide", "narrow"), axis=0, tiled=True),
         lax.all_gather(out_low, ("wide", "narrow"), axis=0, tiled=True),
-        lax.all_gather(up_low, ("wide", "narrow"), axis=0, tiled=True),
+        jnp.concatenate(
+            lax.all_to_all(
+                jnp.stack([up_low] * lax.axis_size(("wide", "narrow"))), ("wide", "narrow"), 0, 0
+            ),
+            axis=0,
+        ),
         lax.all_gather(down_low, ("wide", "narrow"), axis=0, tiled=True),
         lax.all_gather(vec_low, ("wide", "narrow"), axis=0, tiled=True),
     )

time: 1130 us -> 1210 us (1.071)
  blocking collectives: 43.8 us -> 204 us
  waiting for transfers between devices: 965 us -> 877 us
    all_gather x1, blocking collectives: 43.8 us -> 204 us  [body(): lax.all_gather(vec_low, ('wide', 'narrow'), axis=0, tiled=True)]
    all_gather x1, waiting for transfers between devices: 52.9 us -> 0.7 us  [body(): lax.all_gather(out_low, ('wide', 'narrow'), axis=0, tiled=True)]
    all_gather x1, waiting for transfers between devices: 25.6 us -> 0.02 us  [body(): lax.all_gather(qkv_low, ('wide', 'narrow'), axis=0, tiled=True)]
  transfers between devices with their start and end apart: 11 -> 12, of which waited for: 11 -> 11; matrix products, arithmetic and copies ran while one was open for 5% -> 6% of each run, Pallas kernels for 0% -> 0%
where the time goes in v1:
time: 1210 us
  waiting for transfers between devices  877 us (72%)
  blocking collectives  204 us (17%)
  matrix products  62.4 us (5%)
  local copies, waits for them, and re-layouts  24.2 us (2%)
  other arithmetic  23.8 us (2%)
  between operations  14.4 us (1%)
    unnamed x12, waiting for transfers between devices  425 us
    all_gather x1, blocking collectives, body(): lax.all_gather(vec_low, ('wide', 'narrow'), axis=0, tiled=True)  204 us
    reduce_scatter x1, waiting for transfers between devices, body(): lax.psum_scatter(group_sums[3].astype(jnp.bfloat16), 'wide', scatter_dime...  69 us
    all_gather x1, waiting for transfers between devices, body(): lax.all_gather(up_low, ('wide', 'narrow'), axis=0, tiled=True)  68.2 us
    reduce_scatter x1, waiting for transfers between devices, body(): lax.psum_scatter(group_sums[2].astype(jnp.bfloat16), 'wide', scatter_dime...  67.4 us
    reduce_scatter x1, waiting for transfers between devices, body(): lax.psum_scatter(group_sums[0].astype(jnp.bfloat16), 'wide', scatter_dime...  64.9 us
    reduce_scatter x1, waiting for transfers between devices, body(): lax.psum_scatter(group_sums[1].astype(jnp.bfloat16), 'wide', scatter_dime...  63 us
    all_gather x1, waiting for transfers between devices, body(): lax.all_gather(down_low, ('wide', 'narrow'), axis=0, tiled=True)  62.5 us
  transfers between devices with their start and end apart: 12, of which 11 were waited for; matrix products, arithmetic and copies ran while one was open for 6% of the time, Pallas kernels for 0%

profile of v1, /device:TPU:0, one launch (start us, length us, event | category | flops | bytes accessed | tf_op | source)
XLA Modules:
  0.0 1213.8 jit_solution(9089258670706939455)
XLA Ops:
  7.2 1.7 convert_element_type.142
  9.1 1.5 convert_element_type.147
  10.7 1.8 convert_element_type.151
  12.5 4.3 stack.12
  16.8 7.5 all-to-all-start
  24.4 0.5 all-gather.12.cloned.1.call-update
  25.1 204.2 %all-gather = bf16[32,32,12]{1,2,0:T(8,128)(2,1)S(1)} all-gather(bf16[1,32,12]{1,2,0:T(8,128)(2,1)S(1)} %convert_bitcast_fusion.10), channel_id=1, replica_groups=mesh['wide'=8,'narrow'=4] {'wide','narrow'}, dimensions={0}, use_global_device_ids=true | all-gather | bytes 25344 | tf_op jit(solution)/shard_map/all_gather | solution.py:74
  230.0 3.9 fusion
  234.5 0.4 fusion.109
  235.0 0.3 convolution_convert_fusion.6
  235.4 0.7 all-gather.8.cloned.1.call-done
  236.1 2.1 fusion.110
  238.5 7.9 all-to-all-done
  246.4 6.1 convolution_add_fusion
  252.5 62.5 %all-gather.10.cloned.1.call-done = bf16[4096,1024]{1,0:T(8,128)(2,1)} async-done(((bf16[128,1024]{1,0:T(8,128)(2,1)}), bf16[4096,1024]{1,0:T(8,128)(2,1)}) %all-gather.10.cloned.1.call-update) | async-done | bytes 8388624 | tf_op jit(solution)/shard_map/all_gather | solution.py:73
  315.0 10.8 fusion.102
  325.8 68.2 %all-gather.12.cloned.1.call-done = bf16[1024,4096]{1,0:T(8,128)(2,1)} async-done(((bf16[32,4096]{1,0:T(8,128)(2,1)}), bf16[1024,4096]{1,0:T(8,128)(2,1)}) %all-gather.12.cloned.1.call-update) | async-done | bytes 8388624 | tf_op jit(solution)/shard_map/all_gather | solution.py:139
  394.0 6.9 multiply_reduce_fusion.1
  400.9 0.3 fusion.104
  401.2 0.8 convolution_convert_fusion.5
  402.2 0.5 convolution_convert_fusion.4
  402.7 1.3 multiply_reduce_fusion
  404.3 0.5 fusion.12
  405.0 0.3 fusion.11
  405.3 0.3 fusion.87
  405.6 4.7 convolution_convert_fusion.2
  410.2 5.7 convolution_convert_fusion.1
  416.4 5.1 fusion.91
  421.5 0.4 fusion.23
  421.9 1.1 fusion.90
  423.5 0.7 copy.95
  424.5 5.6 convolution_convert_fusion
  430.1 2.1 convolution_convert_fusion.3
  432.3 0.6 copy-done.27
  432.8 0.6 dynamic-slice
  433.4 9.2 reduce-scatter.27.cloned.1.call-done
  442.7 1.4 copy.96
  444.1 424.2 %all-reduce.7.cloned.1.call-done = (bf16[8,4,32,3072]{3,2,1,0:T(8,128)(2,1)}, bf16[8,4,32,1024]{3,2,1,0:T(8,128)(2,1)}, bf16[8,4,32,4096]{3,2,1,0:T(8,128)(2,1)}, bf16[8,4,128,1024]{3,2,1,0:T(8,128)(2,1)}) async-done(((bf16[8,4,32,3072]{3,2,1,0:T(8,128)(2,1)}, bf16[8,4,32,1024]{3,2,1,0:T(8,128)(2,1)}, bf16[8,4,32,4096]{3,2,1,0:T(8,128)(2,1)}, bf16[8,4,128,1024]{3,2,1,0:T(8,128)(2,1)}), ...) | async-done | bytes 25165840
  868.2 2.5 constant_dynamic-slice_fusion.2
  870.8 3.3 constant_dynamic-slice_fusion.3
  874.2 3.8 constant_dynamic-slice_fusion.1
  878.1 0.6 copy-done.25
  878.8 5.4 fusion.10
  884.1 3.8 constant_dynamic-slice_fusion
  887.9 39.0 %reduce-scatter.29.cloned.1.call-done = bf16[1,1,32,12]{2,3,1,0:T(8,128)(2,1)} async-done(((bf16[8,1,32,12]{2,3,1,0:T(8,128)(2,1)}), bf16[1,1,32,12]{2,3,1,0:T(8,128)(2,1)}) %reduce-scatter.29.cloned.1.call-update) | async-done | bytes 784 | tf_op jit(solution)/shard_map/reduce_scatter | solution.py:270
  926.9 0.7 multiply_add_fusion.8
  927.6 0.6 copy.100
  928.2 1.3 fusion.92
  929.5 63.0 %reduce-scatter.21.cloned.1.call-done = bf16[1,1,32,1024]{3,2,1,0:T(8,128)(2,1)} async-done(((bf16[8,1,32,1024]{3,2,1,0:T(8,128)(2,1)}), bf16[1,1,32,1024]{3,2,1,0:T(8,128)(2,1)}) %reduce-scatter.21.cloned.1.call-update) | async-done | bytes 65552 | tf_op jit(solution)/shard_map/reduce_scatter | solution.py:261
  992.5 0.9 multiply_add_fusion.6
  993.4 0.7 pad_maximum_fusion.4
  994.1 1.7 fusion.98
  995.8 64.9 %reduce-scatter.19.cloned.1.call-done = bf16[1,1,32,3072]{3,2,1,0:T(8,128)(2,1)} async-done(((bf16[8,1,32,3072]{3,2,1,0:T(8,128)(2,1)}), bf16[1,1,32,3072]{3,2,1,0:T(8,128)(2,1)}) %reduce-scatter.19.cloned.1.call-update) | async-done | bytes 196624 | tf_op jit(solution)/shard_map/reduce_scatter | solution.py:258
  1060.7 1.1 multiply_add_fusion.4
  1061.9 0.9 pad_maximum_fusion.3
  1062.8 1.1 fusion.100
  1063.9 67.4 %reduce-scatter.23.cloned.1.call-done = bf16[1,1,32,4096]{3,2,1,0:T(8,128)(2,1)} async-done(((bf16[8,1,32,4096]{3,2,1,0:T(8,128)(2,1)}), bf16[1,1,32,4096]{3,2,1,0:T(8,128)(2,1)}) %reduce-scatter.23.cloned.1.call-update) | async-done | bytes 262160 | tf_op jit(solution)/shard_map/reduce_scatter | solution.py:264
  1131.3 1.1 multiply_add_fusion.1
  1132.4 1.0 pad_maximum_fusion
  1133.5 69.0 %reduce-scatter.25.cloned.1.call-done = bf16[1,1,128,1024]{3,2,1,0:T(8,128)(2,1)} async-done(((bf16[8,1,128,1024]{3,2,1,0:T(8,128)(2,1)}), bf16[1,1,128,1024]{3,2,1,0:T(8,128)(2,1)}) %reduce-scatter.25.cloned.1.call-update) | async-done | bytes 262160 | tf_op jit(solution)/shard_map/reduce_scatter | solution.py:267
  1202.5 1.1 multiply_add_fusion
  1203.6 1.1 pad_maximum_fusion.1
  1204.7 1.3 fusion.96
  1206.0 1.3 fusion.94
  (129 shorter events, 4.4 us)
Async XLA Ops:
  7.2 5.3 copy-start.11
  7.2 222.8 %all-gather.6.cloned.1.call-start = ((), (), s32[]{:S(2)}) async-start(), calls=%async_computation.7 | async-start | bytes 6488064 | tf_op jit(solution)/shard_map/all_gather | solution.py:65
  9.0 227.1 %all-gather.8.cloned.1.call-start = ((), (), s32[]{:S(2)}) async-start(), calls=%async_computation.8 | async-start | bytes 2162688 | tf_op jit(solution)/shard_map/all_gather | solution.py:66
  10.6 304.3 %all-gather.10.cloned.1.call-start = ((), (), s32[]{:S(2)}) async-start(), calls=%async_computation.9 | async-start | bytes 8650752 | tf_op jit(solution)/shard_map/all_gather | solution.py:73
  12.5 4.3 copy-start.8
  16.8 8.1 copy-start.3
  16.8 8.3 copy-start.24
  16.8 212.7 %copy-start = (bf16[128,1024]{1,0:T(8,128)(2,1)S(1)}, bf16[128,1024]{1,0:T(8,128)(2,1)}, u32[]{:S(2)}) copy-start(bf16[128,1024]{1,0:T(8,128)(2,1)} %param.13) | copy-start | bytes 786436
  16.8 213.0 %copy-start.26 = (s32[1,128]{1,0:T(1,128)S(1)}, s32[1,128]{1,0:T(1,128)}, u32[]{:S(2)}) copy-start(s32[1,128]{1,0:T(1,128)} %param.15) | copy-start | bytes 1540
  16.8 229.5 %all-to-all-start = ((bf16[32,32,4096]{2,1,0:T(8,128)(2,1)}), bf16[32,32,4096]{2,1,0:T(8,128)(2,1)}, u32[]{:S(2)}, u32[]{:S(2)}) async-start(bf16[32,32,4096]{2,1,0:T(8,128)(2,1)} %stack.12), calls=%async_computation | async-start | bytes 16777216 | tf_op jit(solution)/shard_map/all_to_all | solution.py:68
  24.3 369.7 %all-gather.12.cloned.1.call-start = ((), (), s32[]{:S(2)}) async-start(), calls=%async_computation.10 | async-start | bytes 8650752 | tf_op jit(solution)/shard_map/all_gather | solution.py:139
  24.9 417.8 %reduce-scatter.27.cloned.1.call-start = ((), (), s32[]{:S(2)}) async-start(), calls=%async_computation.15 | async-start | bytes 122880 | tf_op jit(solution)/shard_map/reduce_scatter | solution.py:253
  234.1 1.2 copy-start.9
  234.5 0.9 copy-start.18
  235.4 17.1 %copy-start.20 = (bf16[16,64,128]{2,1,0:T(8,128)(2,1)}, bf16[16,64,128]{2,1,0:T(8,128)(2,1)S(1)}, u32[]{:S(2)}) copy-start(bf16[16,64,128]{2,1,0:T(8,128)(2,1)S(1)} %convolution_convert_fusion.6) | copy-start | bytes 786436
  394.0 7.2 copy-start.2
  404.0 1.0 copy-start.10
  405.5 4.7 copy-start.4
  410.2 5.7 copy-start.1
  410.2 5.7 copy-start.14
  424.2 5.9 copy-start.21
  424.2 444.0 %all-reduce.7.cloned.1.call-start = ((), (), s32[]{:S(2)}) async-start(), calls=%async_computation.17 | async-start | bytes 50331648
  432.2 0.7 copy-start.27
  432.2 494.7 %reduce-scatter.29.cloned.1.call-start = ((), (), s32[]{:S(2)}) async-start(), calls=%async_computation.16 | async-start | bytes 36864 | tf_op jit(solution)/shard_map/reduce_scatter | solution.py:270
  444.0 548.5 %reduce-scatter.21.cloned.1.call-start = ((), (), s32[]{:S(2)}) async-start(), calls=%async_computation.12 | async-start | bytes 589824 | tf_op jit(solution)/shard_map/reduce_scatter | solution.py:261
  870.8 190.0 %reduce-scatter.19.cloned.1.call-start = ((), (), s32[]{:S(2)}) async-start(), calls=%async_computation.11 | async-start | bytes 1769472 | tf_op jit(solution)/shard_map/reduce_scatter | solution.py:258
  874.2 257.2 %reduce-scatter.23.cloned.1.call-start = ((), (), s32[]{:S(2)}) async-start(), calls=%async_computation.13 | async-start | bytes 2359296 | tf_op jit(solution)/shard_map/reduce_scatter | solution.py:264
  878.0 0.7 copy-start.25
  878.1 324.4 %reduce-scatter.25.cloned.1.call-start = ((), (), s32[]{:S(2)}) async-start(), calls=%async_computation.14 | async-start | bytes 2359296 | tf_op jit(solution)/shard_map/reduce_scatter | solution.py:267
  887.9 104.7 %copy-start.19 = (f32[2,32,1024]{2,1,0:T(8,128)S(1)}, f32[2,32,1024]{2,1,0:T(8,128)}, u32[]{:S(2)}) copy-start(f32[2,32,1024]{2,1,0:T(8,128)} %param.22) | copy-start | bytes 786436
  887.9 106.3 %copy-start.23 = (f32[32,1024]{1,0:T(8,128)S(1)}, f32[32,1024]{1,0:T(8,128)}, u32[]{:S(2)}) copy-start(f32[32,1024]{1,0:T(8,128)} %param.17) | copy-start | bytes 393220
  887.9 172.9 %copy-start.7 = (f32[2,32,3072]{2,1,0:T(8,128)S(1)}, f32[2,32,3072]{2,1,0:T(8,128)}, u32[]{:S(2)}) copy-start(f32[2,32,3072]{2,1,0:T(8,128)} %param.21) | copy-start | bytes 2359300
  994.1 68.7 %copy-start.15 = (f32[32,3072]{1,0:T(8,128)S(1)}, f32[32,3072]{1,0:T(8,128)}, u32[]{:S(2)}) copy-start(f32[32,3072]{1,0:T(8,128)} %param.16) | copy-start | bytes 1179652
  1060.7 2.0 copy-start.22
  1061.8 69.5 %copy-start.5 = (f32[2,32,4096]{2,1,0:T(8,128)S(1)}, f32[2,32,4096]{2,1,0:T(8,128)}, u32[]{:S(2)}) copy-start(f32[2,32,4096]{2,1,0:T(8,128)} %param.23) | copy-start | bytes 3145732
  1063.9 138.5 %copy-start.6 = (f32[2,128,1024]{2,1,0:T(8,128)S(1)}, f32[2,128,1024]{2,1,0:T(8,128)}, u32[]{:S(2)}) copy-start(f32[2,128,1024]{2,1,0:T(8,128)} %param.24) | copy-start | bytes 3145732
  1133.5 71.2 %copy-start.12 = (f32[32,4096]{1,0:T(8,128)S(1)}, f32[32,4096]{1,0:T(8,128)}, u32[]{:S(2)}) copy-start(f32[32,4096]{1,0:T(8,128)} %param.18) | copy-start | bytes 1572868
  1133.5 71.2 %copy-start.16 = (bf16[1,1,32,4096]{3,2,1,0:T(8,128)(2,1)S(1)}, bf16[1,1,32,4096]{3,2,1,0:T(8,128)(2,1)}, u32[]{:S(2)}) copy-start(bf16[1,1,32,4096]{3,2,1,0:T(8,128)(2,1)} %reduce-scatter.23.cloned.1.call-done) | copy-start | bytes 786436
  1203.6 2.4 copy-start.13
  1203.6 2.4 copy-start.17
Sparse Core Ops, SparseCore 0:
  11.5 135.1 all-gather.5
  150.1 85.9 all-gather.7
  239.5 75.4 all-gather.9
  318.3 75.6 all-gather.11
  424.3 18.2 reduce-scatter.26
  445.3 422.9 all-reduce.6
  871.9 54.9 reduce-scatter.28
  930.8 61.6 reduce-scatter.20
  995.9 64.7 reduce-scatter.18
  1064.1 67.1 reduce-scatter.22
  1134.9 67.5 reduce-scatter.24
